TPU v7x, 256 devices: a whole 4x4x8 slice. The times are simulated.
256 devices in a mesh: blk: 128 (over y, z, x_lo, core), rel: 2 (over x_hi).
Axes of the slice: x: 4 (x_hi: 2, x_lo: 2; x = x_hi * 2 + x_lo), y: 4, z: 8, core: 2. Of those that a mesh axis runs over, the one named last changes fastest.
Arguments:
- user_table: float32 [131072, 512], P(('blk', 'rel')), may hold values from -1.5 to 1.5
- user_accum: float32 [131072], P(('blk', 'rel')), may hold values from 1 to 100
- item_table: float32 [262144, 512], P(('blk', 'rel')), may hold values from -1.5 to 1.5
- item_accum: float32 [262144], P(('blk', 'rel')), may hold values from 1 to 100
- relation: bfloat16 [512, 512], replicated, may hold values from -0.25 to 0.25
- relation_accum: float32 [512], replicated, may hold values from 0.5 to 8
- targets: bfloat16 [2, 131072, 2048], P(None, 'blk', 'rel'), may hold values from 0 to 1
Outputs:
- user_table_next: float32 [131072, 512], P(('blk', 'rel'))
- user_accum_next: float32 [131072], P(('blk', 'rel'))
- item_table_next: float32 [262144, 512], P(('blk', 'rel'))
- item_accum_next: float32 [262144], P(('blk', 'rel'))
- relation_step: float32 [512, 512], replicated
- relation_accum_next: float32 [512], replicated
All inputs are finite; a program needn't handle non-finite values.
Results may differ from a plain program's by a relative error of at most 0.0037.
The roundings to bfloat16 on the way count: a program that leaves them out, or rounds other values in their place, can miss the bound.
Values may be sent and summed in bfloat16 or wider, within the bound.
A program may use at most 64 MiB of HBM per device.

v0:
```python
import jax
import jax.numpy as jnp
from jax import lax
from jax.sharding import PartitionSpec as P

learn_rate = 0.1
epsilon = 1e-06


def from_everyone(shard, axis):
    copies = jnp.broadcast_to(shard, (lax.axis_size(axis), *shard.shape))
    return lax.all_to_all(copies, axis, split_axis=0, concat_axis=0, tiled=True)


def in_order(pieces, dim):
    pieces = jnp.moveaxis(pieces, 0, dim)
    dims = pieces.shape
    return pieces.reshape(*dims[:dim], dims[dim] * dims[dim + 1], *dims[dim + 2 :])


def collect(shard, axis, dim):
    pieces = from_everyone(shard, axis)
    return in_order(pieces, dim)


def in_blocks(shard, dim, peers):
    before, after = (shard.shape[:dim], shard.shape[dim + 1 :])
    return jnp.moveaxis(shard.reshape(*before, peers, -1, *after), dim, 0)


def sum_at_owner(shard, axis, dim):
    peers = lax.axis_size(axis)
    pieces = lax.all_to_all(in_blocks(shard, dim, peers), axis, 0, 0, tiled=True)
    return jnp.sum(pieces, axis=0)


def from_behind(shard, axis, by):
    peers = lax.axis_size(axis)
    return lax.ppermute(shard, axis, [(i, (i + by) % peers) for i in range(peers)])


def adagrad_rows(table, accum, grads):
    accum_next = accum + jnp.mean(grads * grads, axis=1)
    return (table - learn_rate * grads * lax.rsqrt(accum_next + epsilon)[:, None], accum_next)


def per_device(user_table, user_accum, item_table, item_accum, relation, relation_accum, targets):
    blocks = lax.axis_size("blk")
    rounds = targets.shape[0]
    users_now, user_sums = (user_table, user_accum)
    items_now, item_sums = (item_table, item_accum)
    relation_local = jnp.zeros((relation.shape[0], relation.shape[1]), jnp.float32)
    for turn in range(rounds):
        whole_users = collect(users_now.astype(jnp.bfloat16), "rel", 0)
        item_bf = items_now.astype(jnp.bfloat16)
        anchor = jnp.dot(whole_users, relation, preferred_element_type=jnp.float32).astype(
            jnp.bfloat16
        )
        scores = lax.dot_general(
            anchor, item_bf, (((1,), (1,)), ((), ())), preferred_element_type=jnp.float32
        )
        errors = (jax.nn.sigmoid(scores) - targets[turn].astype(jnp.float32)).astype(jnp.bfloat16)
        mapped = lax.dot_general(
            item_bf, relation, (((1,), (1,)), ((), ())), preferred_element_type=jnp.float32
        ).astype(jnp.bfloat16)
        user_grad = sum_at_owner(
            jnp.dot(errors, mapped, preferred_element_type=jnp.float32), "rel", 0
        )
        item_grad = lax.dot_general(
            errors, anchor, (((0,), (0,)), ((), ())), preferred_element_type=jnp.float32
        )
        crossed = lax.dot_general(
            whole_users, errors, (((0,), (0,)), ((), ())), preferred_element_type=jnp.float32
        ).astype(jnp.bfloat16)
        term = jnp.dot(crossed, item_bf, preferred_element_type=jnp.float32)
        relation_local = relation_local + term
        users_now, user_sums = adagrad_rows(users_now, user_sums, user_grad)
        items_now, item_sums = adagrad_rows(items_now, item_sums, item_grad)
        items_now, item_sums = from_behind((items_now, item_sums), "blk", 1)
    total = lax.psum(relation_local, ("blk", "rel"))
    mean_grad = total / (blocks * rounds)
    accum_next = relation_accum + jnp.mean(mean_grad * mean_grad, axis=1)
    relation_step = mean_grad * lax.rsqrt(accum_next + epsilon)[:, None]
    return (users_now, user_sums, items_now, item_sums, relation_step, accum_next)


def solution(mesh):
    return jax.shard_map(
        per_device,
        mesh=mesh,
        in_specs=(
            P(("blk", "rel"), None),
            P(("blk", "rel")),
            P(("blk", "rel"), None),
            P(("blk", "rel")),
            P(),
            P(),
            P(None, "blk", "rel"),
        ),
        out_specs=(
            P(("blk", "rel"), None),
            P(("blk", "rel")),
            P(("blk", "rel"), None),
            P(("blk", "rel")),
            P(),
            P(),
        ),
        check_vma=False,
    )
```

profile of v0, /device:TPU:2, one launch (start us, length us, event | category | flops | bytes accessed | tf_op | source)
XLA Modules:
  0.0 427.7 jit_solution(13035519853064472672)
XLA Ops:
  7.2 0.0 copy-start
  7.2 1.4 convert_element_type.49
  8.5 1.0 broadcast_in_dim.4
  9.6 4.5 %all-to-all-start = ((bf16[2,512,512]{2,1,0:T(8,128)(2,1)}), bf16[2,512,512]{2,1,0:T(8,128)(2,1)}, u32[]{:S(2)}, u32[]{:S(2)}) async-start(bf16[2,512,512]{2,1,0:T(8,128)(2,1)} %broadcast_in_dim.4), calls=%async_computation | async-start | bytes 2097152 | tf_op jit(solution)/shard_map/all_to_all | solution.py:12
  14.0 1.9 copy.13
  16.0 13.5 %all-to-all-done = bf16[2,512,512]{2,1,0:T(8,128)(2,1)} async-done(((bf16[2,512,512]{2,1,0:T(8,128)(2,1)}), bf16[2,512,512]{2,1,0:T(8,128)(2,1)}, u32[]{:S(2)}, u32[]{:S(2)}) %all-to-all-start) | async-done | bytes 1048608 | tf_op jit(solution)/shard_map/all_to_all | solution.py:12
  29.5 2.1 convolution_convert_fusion.5
  31.6 3.3 fusion.1
  34.9 0.0 copy-start.7
  34.9 1.3 copy-done.7
  36.2 2.7 multiply_reduce_fusion.1
  38.9 5.4 %fusion.2 = f32[1024,512]{1,0:T(8,128)} fusion(bf16[1024,1024]{1,0:T(8,128)(2,1)} %copy-done.7, bf16[512,512]{1,0:T(8,128)(2,1)S(1)} %copy-done, f32[1024,512]{1,0:T(8,128)} %param.9), kind=kOutput, calls=%fused_computation.20 | convolution fusion | flops 1611661312 | bytes 6815744 | tf_op jit(solution)/shard_map/dot_general | solution.py:67
  44.3 4.9 %all-to-all-start.1 = ((f32[2,512,512]{2,1,0:T(8,128)}), f32[2,512,512]{2,1,0:T(8,128)}, u32[]{:S(2)}, u32[]{:S(2)}) async-start(f32[2,512,512]{2,1,0:T(8,128)} %bitcast.29), calls=%async_computation.1 | async-start | bytes 4194304 | tf_op jit(solution)/shard_map/all_to_all | solution.py:33
  49.3 3.5 multiply_subtract_fusion.1
  52.8 0.0 collective-permute-start
  52.8 44.8 %all-to-all-done.1 = f32[2,512,512]{2,1,0:T(8,128)} async-done(((f32[2,512,512]{2,1,0:T(8,128)}), f32[2,512,512]{2,1,0:T(8,128)}, u32[]{:S(2)}, u32[]{:S(2)}) %all-to-all-start.1) | async-done | bytes 2097184 | tf_op jit(solution)/shard_map/all_to_all | solution.py:33
  97.6 1.9 reduce_sum.63
  99.4 0.1 multiply_reduce_fusion.4
  99.6 0.2 fusion.5
  99.8 1.0 broadcast_in_dim.5
  100.8 4.4 %all-to-all-start.2 = ((bf16[2,512,512]{2,1,0:T(8,128)(2,1)}), bf16[2,512,512]{2,1,0:T(8,128)(2,1)}, u32[]{:S(2)}, u32[]{:S(2)}) async-start(bf16[2,512,512]{2,1,0:T(8,128)(2,1)} %broadcast_in_dim.5), calls=%async_computation.2 | async-start | bytes 2097152 | tf_op jit(solution)/shard_map/all_to_all | solution.py:12
  105.3 0.0 all-reduce.2.cloned.1.call-start
  105.3 0.3 collective-permute-start.1
  105.6 5.3 %fusion.4 = f32[512,512]{1,0:T(8,128)} fusion(bf16[1024,1024]{1,0:T(8,128)(2,1)} %copy-done.7, bf16[1024,512]{1,0:T(8,128)(2,1)} %bitcast, f32[1024,512]{1,0:T(8,128)} %param.9), kind=kOutput, calls=%fused_computation.22 | convolution fusion | flops 1611661312 | bytes 6291456 | tf_op jit(solution)/shard_map/dot_general | solution.py:75
  110.9 8.1 %all-to-all-done.2 = bf16[2,512,512]{2,1,0:T(8,128)(2,1)} async-done(((bf16[2,512,512]{2,1,0:T(8,128)(2,1)}), bf16[2,512,512]{2,1,0:T(8,128)(2,1)}, u32[]{:S(2)}, u32[]{:S(2)}) %all-to-all-start.2) | async-done | bytes 1048608 | tf_op jit(solution)/shard_map/all_to_all | solution.py:12
  119.1 1.9 convolution_convert_fusion.3
  121.0 0.0 copy-start.6
  121.0 0.0 collective-permute-done
  121.0 0.9 copy-done.6
  122.0 5.2 %fusion = bf16[1024,1024]{1,0:T(8,128)(2,1)} fusion(bf16[1024,512]{1,0:T(8,128)(2,1)S(1)} %convolution_convert_fusion.3, bf16[2,1024,1024]{2,1,0:T(8,128)(2,1)} %param.13, f32[1024,512]{0,1:T(8,128)} %collective-permute-done), kind=kOutput, calls=%fused_computation.1 | convolution fusion | flops 1080557568 | bytes 7340032 | tf_op jit(solution)/shard_map/dot_general | solution.py:59
  127.2 5.6 %convolution_add_fusion = f32[512,512]{1,0:T(8,128)} fusion(f32[512,512]{1,0:T(8,128)} %fusion.4, bf16[1024,512]{1,0:T(8,128)(2,1)} %bitcast.3, bf16[1024,1024]{1,0:T(8,128)(2,1)} %fusion, f32[1024,512]{0,1:T(8,128)} %collective-permute-done), kind=kOutput, calls=%fused_computation.14 | convolution fusion | flops 1611923456 | bytes 7340032 | tf_op jit(solution)/shard_map/dot_general | solution.py:75
  132.8 4.5 %multiply_reduce_fusion = (f32[1024]{0:T(1024)S(1)}, f32[1024,512]{0,1:T(8,128)}) fusion(bf16[1024,1024]{1,0:T(8,128)(2,1)} %fusion, bf16[1024,512]{1,0:T(8,128)(2,1)} %copy-done.6), kind=kOutput, calls=%fused_computation.5 | convolution fusion | flops 1074789376 | bytes 5246976 | tf_op jit(solution)/shard_map/dot_general | solution.py:69
  137.2 0.0 all-reduce.2.cloned.1.call-update
  137.3 4.2 multiply_subtract_fusion
  141.4 5.4 %fusion.3 = f32[1024,512]{1,0:T(8,128)} fusion(bf16[1024,1024]{1,0:T(8,128)(2,1)} %fusion, bf16[512,512]{1,0:T(8,128)(2,1)S(1)} %copy-done, f32[1024,512]{0,1:T(8,128)} %collective-permute-done), kind=kOutput, calls=%fused_computation.21 | convolution fusion | flops 1611661312 | bytes 6815744 | tf_op jit(solution)/shard_map/dot_general | solution.py:67
  146.8 5.0 %all-to-all-start.3 = ((f32[2,512,512]{2,1,0:T(8,128)}), f32[2,512,512]{2,1,0:T(8,128)}, u32[]{:S(2)}, u32[]{:S(2)}) async-start(f32[2,512,512]{2,1,0:T(8,128)} %bitcast.28), calls=%async_computation.3 | async-start | bytes 4194304 | tf_op jit(solution)/shard_map/all_to_all | solution.py:33
  151.8 0.1 collective-permute-start.3
  151.9 38.7 %collective-permute-done.3 = f32[1024]{0:T(1024)S(1)} collective-permute-done((f32[1024]{0:T(1024)S(1)}, f32[1024]{0:T(1024)S(1)}, u32[]{:S(2)}, u32[]{:S(2)}) %collective-permute-start.3) | collective-permute-done | bytes 4128 | tf_op jit(solution)/shard_map/ppermute | solution.py:39
  190.7 215.1 %all-reduce.2.cloned.1.call-done = f32[512,512]{1,0:T(8,128)} async-done(((f32[512,512]{1,0:T(8,128)}), f32[512,512]{1,0:T(8,128)}) %all-reduce.2.cloned.1.call-update) | async-done | bytes 1048592 | tf_op jit(solution)/shard_map/psum | solution.py:80
  405.8 1.4 multiply_reduce_fusion.2
  407.2 0.6 rsqrt_multiply_fusion.2
  407.8 2.3 broadcast_multiply_fusion
  410.1 2.9 reduce_sum.66
  413.0 1.4 multiply_reduce_fusion.3
  414.4 0.6 rsqrt_multiply_fusion.3
  414.9 2.4 multiply_subtract_fusion.2
  417.4 2.9 copy.14
  420.3 0.6 copy.17
  (18 shorter events, 0.1 us)
Async XLA Ops:
  7.2 22.3 %copy-start = (bf16[512,512]{1,0:T(8,128)(2,1)S(1)}, bf16[512,512]{1,0:T(8,128)(2,1)}, u32[]{:S(2)}) copy-start(bf16[512,512]{1,0:T(8,128)(2,1)} %param.11) | copy-start | bytes 1572868
  9.6 19.9 %all-to-all-start = ((bf16[2,512,512]{2,1,0:T(8,128)(2,1)}), bf16[2,512,512]{2,1,0:T(8,128)(2,1)}, u32[]{:S(2)}, u32[]{:S(2)}) async-start(bf16[2,512,512]{2,1,0:T(8,128)(2,1)} %broadcast_in_dim.4), calls=%async_computation | async-start | bytes 2097152 | tf_op jit(solution)/shard_map/all_to_all | solution.py:12
  29.5 2.1 copy-start.2
  34.9 1.3 copy-start.7
  44.3 5.0 %copy-start.4 = (f32[1024]{0:T(1024)S(1)}, f32[1024]{0:T(1024)}, u32[]{:S(2)}) copy-start(f32[1024]{0:T(1024)} %param.10) | copy-start | bytes 12292
  44.3 53.3 %all-to-all-start.1 = ((f32[2,512,512]{2,1,0:T(8,128)}), f32[2,512,512]{2,1,0:T(8,128)}, u32[]{:S(2)}, u32[]{:S(2)}) async-start(f32[2,512,512]{2,1,0:T(8,128)} %bitcast.29), calls=%async_computation.1 | async-start | bytes 4194304 | tf_op jit(solution)/shard_map/all_to_all | solution.py:33
  52.8 46.8 %copy-start.3 = (f32[512]{0:T(512)S(1)}, f32[512]{0:T(512)}, u32[]{:S(2)}) copy-start(f32[512]{0:T(512)} %param.8) | copy-start | bytes 6148
  52.8 46.8 %copy-start.1 = (f32[512,512]{1,0:T(8,128)S(1)}, f32[512,512]{1,0:T(8,128)}, u32[]{:S(2)}) copy-start(f32[512,512]{1,0:T(8,128)} %param.7) | copy-start | bytes 3145732
  52.8 68.2 %collective-permute-start = (f32[1024,512]{0,1:T(8,128)}, f32[1024,512]{0,1:T(8,128)}, u32[]{:S(2)}, u32[]{:S(2)}) collective-permute-start(f32[1024,512]{0,1:T(8,128)} %multiply_subtract_fusion.1), channel_id=1, source_target_pairs={{0,2},{2,4},{4,6},{6,8},{8,10},{10,12},{12,14},{14,16},{16,18},{18... | collective-permute-start | bytes 6291464 | tf_op jit(solution)/shard_map/ppermute | solution.py:39
  100.8 18.2 %all-to-all-start.2 = ((bf16[2,512,512]{2,1,0:T(8,128)(2,1)}), bf16[2,512,512]{2,1,0:T(8,128)(2,1)}, u32[]{:S(2)}, u32[]{:S(2)}) async-start(bf16[2,512,512]{2,1,0:T(8,128)(2,1)} %broadcast_in_dim.5), calls=%async_computation.2 | async-start | bytes 2097152 | tf_op jit(solution)/shard_map/all_to_all | solution.py:12
  105.3 300.5 %all-reduce.2.cloned.1.call-start = ((), (), s32[]{:S(2)}) async-start(), calls=%async_computation.4 | async-start | bytes 2097152 | tf_op jit(solution)/shard_map/psum | solution.py:80
  105.3 31.9 %collective-permute-start.1 = (f32[1024]{0:T(1024)S(1)}, f32[1024]{0:T(1024)S(1)}, u32[]{:S(2)}, u32[]{:S(2)}) collective-permute-start(f32[1024]{0:T(1024)S(1)} %get-tuple-element.19), channel_id=1, source_target_pairs={{0,2},{2,4},{4,6},{6,8},{8,10},{10,12},{12,14},{14,16},{16,18},{18... | collective-permute-start | bytes 12296 | tf_op jit(solution)/shard_map/ppermute | solution.py:39
  121.0 1.0 copy-start.6
  141.4 275.9 %collective-permute-start.2 = (f32[1024,512]{0,1:T(8,128)}, f32[1024,512]{0,1:T(8,128)}, u32[]{:S(2)}, u32[]{:S(2)}) collective-permute-start(f32[1024,512]{0,1:T(8,128)} %multiply_subtract_fusion), channel_id=1, source_target_pairs={{0,2},{2,4},{4,6},{6,8},{8,10},{10,12},{12,14},{14,16},{16,18},{18... | collective-permute-start | bytes 6291464 | tf_op jit(solution)/shard_map/ppermute | solution.py:39
  146.8 260.4 %copy-start.5 = (f32[512]{0:T(512)S(1)}, f32[512]{0:T(512)}, u32[]{:S(2)}) copy-start(f32[512]{0:T(512)} %param.12) | copy-start | bytes 6148
  146.8 263.3 %all-to-all-start.3 = ((f32[2,512,512]{2,1,0:T(8,128)}), f32[2,512,512]{2,1,0:T(8,128)}, u32[]{:S(2)}, u32[]{:S(2)}) async-start(f32[2,512,512]{2,1,0:T(8,128)} %bitcast.28), calls=%async_computation.3 | async-start | bytes 4194304 | tf_op jit(solution)/shard_map/all_to_all | solution.py:33
  151.8 38.8 %collective-permute-start.3 = (f32[1024]{0:T(1024)S(1)}, f32[1024]{0:T(1024)S(1)}, u32[]{:S(2)}, u32[]{:S(2)}) collective-permute-start(f32[1024]{0:T(1024)S(1)} %get-tuple-element.15), channel_id=1, source_target_pairs={{0,2},{2,4},{4,6},{6,8},{8,10},{10,12},{12,14},{14,16},{16,18},{18... | collective-permute-start | bytes 12296 | tf_op jit(solution)/shard_map/ppermute | solution.py:39
Sparse Core Ops, SparseCore 0:
  137.4 268.3 all-reduce.1
where the time goes:
time: 429 us; the launch traced here: 428 us
  waiting for transfers between devices  320 us (75%)
  matrix products  41.4 us (10%)
  other arithmetic  22.8 us (5%)
  starting transfers between devices  19.2 us (4%)
  between operations  14.2 us (3%)
  local copies, waits for them, and re-layouts  9.78 us (2%)
    psum x1, waiting for transfers between devices, per_device(): total = lax.psum(relation_local, ('blk', 'rel'))  215 us
    all_to_all x2, waiting for transfers between devices, sum_at_owner(): lax.all_to_all(in_blocks(shard, dim, peers), axis, 0, 0, tiled=True)  44.8 us
    ppermute x4, waiting for transfers between devices, from_behind(): lax.ppermute(shard, axis, [(i, (i + by) % peers) for i in range(peers)])  38.8 us
    all_to_all x2, waiting for transfers between devices, from_everyone(): return lax.all_to_all(copies, axis, split_axis=0, concat_axis=0, tiled=True)  21.7 us
    dot_general x2, matrix products, per_device(): term = jnp.dot(crossed, item_bf, preferred_element_type=jnp.float32)  10.9 us
    dot_general x2, matrix products, per_device(): jnp.dot(errors, mapped, preferred_element_type=jnp.float32)  10.8 us
    sub x3, other arithmetic, adagrad_rows(): table - learn_rate * grads * lax.rsqrt(accum_next + epsilon)[:, None]  10.1 us
    all_to_all x2, starting transfers between devices, sum_at_owner(): lax.all_to_all(in_blocks(shard, dim, peers), axis, 0, 0, tiled=True)  9.91 us
  transfers between devices with their start and end apart: 9, of which 5 were waited for; matrix products, arithmetic and copies ran while one was open for 12% of the time, Pallas kernels for 0%

commit v1 on v0

v1 whole, which is shorter than its diff:
```python
import jax
import jax.numpy as jnp
from jax import lax
from jax.experimental import pallas as pl
from jax.experimental.pallas import tpu as pltpu
from jax.sharding import PartitionSpec as P

learn_rate = 0.1
epsilon = 1e-06

MESH = pl.DeviceIdType.MESH
D = 512
UH = 512
IH = 1024
NB = 128
ROUNDS = 2
UC = 128
IC = 256
BF = jnp.bfloat16
F32 = jnp.float32


def mm(a, b, ca, cb):
    return lax.dot_general(a, b, (((ca,), (cb,)), ((), ())), preferred_element_type=F32)


def to_columns(rows, cols):
    for i in range(rows.shape[0]):
        cols[i * 128 : (i + 1) * 128, :] = jnp.broadcast_to(rows[i : i + 1, :], (128, 128)).T


def to_rows(cols, rows):
    for i in range(rows.shape[0]):
        rows[i : i + 1, :] = cols[i * 128 : (i + 1) * 128, :].T[0:1, :]


def adagrad(table, accum, grads):
    accum_next = accum + jnp.mean(grads * grads, axis=1, keepdims=True)
    return table - learn_rate * grads * lax.rsqrt(accum_next + epsilon), accum_next


def kernel(
    user_in, uacc_in, item_in, iacc_in, rel_in, racc_in, tgt_in,
    user_out, uacc_out, item_out, iacc_out, step_out, racc_out,
    users, uacc, items0, items1, items2, iacc0, iacc1, iacc2, rel, racc, tgt0, tgt1,
    ub0, ub1, vb0, vb1, vb2, vtx0, vtx1, anchor, errors, wsum, ugown,
    gtx0, gtx1, grx0, grx1, ucol, icol, rcol, term, rcore, ry, rz, rx, total,
    load, store, usend, urecv, gsend, grecv, isend, irecv, asend, arecv,
    csend, crecv, ysend, yrecv, zsend, zrecv, xsend, xrecv,
):
    b = lax.axis_index("blk")
    r = lax.axis_index("rel")
    core = lax.rem(b, 2)
    xlo = lax.rem(b // 2, 2)
    z = lax.rem(b // 4, 8)
    y = b // 32
    x = 2 * r + xlo
    partner = (b, 1 - r)
    sibling = (b + 1 - 2 * core, r)
    other = (lax.rem(b + 2 * core + (NB - 1), NB), r)
    nxt = (lax.rem(b + 1, NB), r)

    def xpeer(d):
        xp = lax.rem(x + d, 4)
        return (b - 2 * xlo + 2 * lax.rem(xp, 2), xp // 2)

    def ypeer(d):
        return (b - 32 * y + 32 * lax.rem(y + d, 4), r)

    def zpeer(d):
        return (b - 4 * z + 4 * lax.rem(z + d, 8), r)

    barrier = pltpu.get_barrier_semaphore()
    greet = [xpeer(d) for d in range(1, 4)] + [ypeer(d) for d in range(1, 4)]
    greet += [zpeer(d) for d in range(1, 8)] + [sibling, other]
    for peer in greet:
        pl.semaphore_signal(barrier, inc=1, device_id=peer, device_id_type=MESH)

    loads = []
    for src, dst in (
        (user_in, users), (rel_in, rel), (item_in, items0), (tgt_in.at[0], tgt0),
        (uacc_in, uacc), (iacc_in, iacc0), (racc_in, racc), (tgt_in.at[1], tgt1),
    ):
        copy = pltpu.make_async_copy(src, dst, load.at[len(loads)])
        copy.start()
        loads.append(copy)

    own = pl.multiple_of(r * UH, UH)
    far = pl.multiple_of((1 - r) * UH, UH)

    ubs, vbs, vtxs = (ub0, ub1), (vb0, vb1), (vtx0, vtx1)
    tgts, gtxs, grxs = (tgt0, tgt1), (gtx0, gtx1), (grx0, grx1)
    itabs, iaccs, vins = (items0, items1, items2), (iacc0, iacc1, iacc2), (vb0, vb1, vb2)

    def user_copy(turn, k, src0, dst0):
        return pltpu.make_async_remote_copy(
            ubs[turn].at[pl.ds(src0 + k * UC, UC)], ubs[turn].at[pl.ds(dst0 + k * UC, UC)],
            usend.at[turn, k], urecv.at[turn, k], device_id=partner, device_id_type=MESH,
        )

    def grad_copy(turn, k):
        rows = pl.ds(k * UC, UC)
        return pltpu.make_async_remote_copy(
            gtxs[turn].at[rows], grxs[turn].at[rows],
            gsend.at[turn, k], grecv.at[turn, k], device_id=partner, device_id_type=MESH,
        )

    def item_copy_wide(turn, k, src):
        rows = pl.ds(k * IC, IC)
        return pltpu.make_async_remote_copy(
            src.at[rows], itabs[turn + 1].at[rows],
            isend.at[turn, k], irecv.at[turn, k], device_id=nxt, device_id_type=MESH,
        )

    def item_copy(turn, k):
        rows = pl.ds(k * IC, IC)
        return pltpu.make_async_remote_copy(
            vtxs[turn].at[rows], vins[turn + 1].at[rows],
            isend.at[turn, k], irecv.at[turn, k], device_id=nxt, device_id_type=MESH,
        )

    def accum_copy(turn, src):
        return pltpu.make_async_remote_copy(
            src, iaccs[turn + 1], asend.at[turn], arecv.at[turn],
            device_id=nxt, device_id_type=MESH,
        )

    def score_rows(turn, row0, n):
        rows = pl.ds(row0, n)
        anc = mm(ubs[turn][rows, :], rel[...], 1, 0).astype(BF)
        anchor[rows, :] = anc
        scores = mm(anc, vbs[turn][...], 1, 1)
        err = (0.5 * jnp.tanh(0.5 * scores) + 0.5 - tgts[turn][rows, :].astype(F32)).astype(BF)
        errors[rows, :] = err
        w = mm(err, vbs[turn][...], 1, 0).astype(BF)
        wsum[rows, :] = w
        return mm(w, rel[...], 1, 1)

    def own_rows(turn):
        def step(k, carry):
            row0 = pl.multiple_of(k * 256, 256)
            ugown[pl.ds(row0, 256), :] = score_rows(turn, pl.multiple_of(own + row0, 256), 256)
            return carry

        lax.fori_loop(0, UH // 256, step, 0)

    def far_rows(turn):
        def step(k, carry):
            user_copy(turn, k, own, far).wait_recv()
            row0 = pl.multiple_of(k * UC, UC)
            grad = score_rows(turn, pl.multiple_of(far + row0, UC), UC)
            gtxs[turn][pl.ds(row0, UC), :] = grad.astype(BF)
            grad_copy(turn, k).start()
            return carry

        lax.fori_loop(0, UH // UC, step, 0)

    def add_term(turn, row0, first):
        rows = pl.ds(row0, UH)
        part = mm(ubs[turn][rows, :], wsum[rows, :], 0, 0)
        term[...] = part if first else term[...] + part

    def item_chunk(turn, k):
        rows = pl.ds(k * IC, IC)
        grad = mm(errors[:, k * IC : (k + 1) * IC], anchor[...], 0, 0)
        new, acc = adagrad(itabs[turn][rows, :], icol[rows, 0:1], grad)
        icol[rows, :] = jnp.broadcast_to(acc, (IC, 128))
        itabs[turn][rows, :] = new
        vtxs[turn][rows, :] = new.astype(BF)

        @pl.when(core == 0)
        def _():
            item_copy_wide(turn, k, itabs[turn]).start()

        @pl.when(core == 1)
        def _():
            item_copy(turn, k).start()

    def user_chunks(turn):
        def step(k, carry):
            grad_copy(turn, k).wait_recv()
            row0 = pl.multiple_of(k * UC, UC)
            rows = pl.ds(row0, UC)
            grad = ugown[rows, :] + grxs[turn][rows, :].astype(F32)
            new, acc = adagrad(users[rows, :], ucol[rows, 0:1], grad)
            ucol[rows, :] = jnp.broadcast_to(acc, (UC, 128))
            users[rows, :] = new
            if turn + 1 < ROUNDS:
                ubs[turn + 1][pl.ds(pl.multiple_of(own + row0, UC), UC), :] = new.astype(BF)
                user_copy(turn + 1, k, own, own).start()
            return carry

        lax.fori_loop(0, UH // UC, step, 0)

    def items_arrive(turn):
        def step(k, carry):
            row0 = pl.multiple_of(k * IC, IC)
            rows = pl.ds(row0, IC)

            @pl.when(core == 0)
            def _():
                item_copy(turn, k).wait_recv()
                itabs[turn + 1][rows, :] = vins[turn + 1][rows, :].astype(F32)

            @pl.when(core == 1)
            def _():
                item_copy_wide(turn, k, itabs[turn]).wait_recv()
                if turn + 1 < ROUNDS:
                    vins[turn + 1][rows, :] = itabs[turn + 1][rows, :].astype(BF)

            return carry

        lax.fori_loop(0, IH // IC, step, 0)
        accum_copy(turn, iaccs[turn]).wait_recv()

    loads[0].wait()
    ub0[pl.ds(own, UH), :] = users[...].astype(BF)
    pl.semaphore_wait(barrier, len(greet))
    for k in range(UH // UC):
        user_copy(0, k, own, own).start()
    for copy in loads[1:7]:
        copy.wait()
    vb0[...] = items0[...].astype(BF)
    to_columns(uacc, ucol)
    to_columns(iacc0, icol)
    to_columns(racc, rcol)
    own_rows(0)
    add_term(0, own, True)
    far_rows(0)
    for k in range(IH // IC):
        item_chunk(0, k)
    to_rows(icol, iacc0)
    accum_copy(0, iacc0).start()
    user_chunks(0)
    add_term(0, far, False)
    loads[7].wait()

    items_arrive(0)
    to_columns(iacc1, icol)
    own_rows(1)
    add_term(1, own, False)
    far_rows(1)
    add_term(1, far, False)

    half = pl.multiple_of(core * 256, 256)
    away = pl.multiple_of(256 - core * 256, 256)
    base_y = pl.multiple_of(half + y * 64, 64)
    base_z = pl.multiple_of(base_y + z * 8, 8)

    core_copy = pltpu.make_async_remote_copy(
        term.at[pl.ds(away, 256)], rcore, csend.at[0], crecv.at[0],
        device_id=sibling, device_id_type=MESH,
    )
    core_copy.start()
    item_chunk(1, 0)
    core_copy.wait_recv()
    term[pl.ds(half, 256), :] = term[pl.ds(half, 256), :] + rcore[...]
    y_copies = []
    for d in range(1, 4):
        piece = pl.multiple_of(half + lax.rem(y + d, 4) * 64, 64)
        y_copies.append(pltpu.make_async_remote_copy(
            term.at[pl.ds(piece, 64)], ry.at[d - 1], ysend.at[d - 1], yrecv.at[d - 1],
            device_id=ypeer(d), device_id_type=MESH,
        ))
        y_copies[-1].start()
    item_chunk(1, 1)
    item_chunk(1, 2)
    for copy in y_copies:
        copy.wait_recv()
    term[pl.ds(base_y, 64), :] = term[pl.ds(base_y, 64), :] + ry[0] + ry[1] + ry[2]
    z_copies = []
    for d in range(1, 8):
        piece = pl.multiple_of(base_y + lax.rem(z + d, 8) * 8, 8)
        z_copies.append(pltpu.make_async_remote_copy(
            term.at[pl.ds(piece, 8)], rz.at[d - 1], zsend.at[d - 1], zrecv.at[d - 1],
            device_id=zpeer(d), device_id_type=MESH,
        ))
        z_copies[-1].start()
    item_chunk(1, 3)
    to_rows(icol, iacc1)
    accum_copy(1, iacc1).start()
    for copy in z_copies:
        copy.wait_recv()
    part = term[pl.ds(base_z, 8), :]
    for d in range(7):
        part = part + rz[d]
    rx[pl.ds(x, 1)] = part[None]
    x_sends, x_recvs = [], []
    for d in range(1, 4):
        args = dict(send_sem=xsend.at[d - 1], recv_sem=xrecv.at[d - 1],
                    device_id=xpeer(d), device_id_type=MESH)
        x_sends.append(pltpu.make_async_remote_copy(rx.at[x], rx.at[x], **args))
        x_recvs.append(pltpu.make_async_remote_copy(rx.at[x], rx.at[lax.rem(x + 4 - d, 4)], **args))
        x_sends[-1].start()

    user_chunks(1)
    to_rows(ucol, uacc)
    stores = [
        pltpu.make_async_copy(users, user_out, store.at[0]),
        pltpu.make_async_copy(uacc, uacc_out, store.at[1]),
    ]
    for copy in stores:
        copy.start()

    for copy in x_recvs:
        copy.wait_recv()
    total[pl.ds(base_z, 8), :] = rx[0] + rx[1] + rx[2] + rx[3]

    def spread(src0, dst0, n, sends, recvs, k, peer):
        return pltpu.make_async_remote_copy(
            total.at[pl.ds(src0, n)], total.at[pl.ds(dst0, n)], sends.at[k], recvs.at[k],
            device_id=peer, device_id_type=MESH,
        )

    back = []
    for d in range(1, 8):
        back.append(spread(base_z, base_z, 8, zsend, zrecv, 6 + d, zpeer(d)))
        back[-1].start()
    for d in range(1, 8):
        src = pl.multiple_of(base_y + lax.rem(z + 8 - d, 8) * 8, 8)
        spread(base_z, src, 8, zsend, zrecv, 6 + d, zpeer(d)).wait_recv()
    for d in range(1, 4):
        back.append(spread(base_y, base_y, 64, ysend, yrecv, 2 + d, ypeer(d)))
        back[-1].start()
    for d in range(1, 4):
        src = pl.multiple_of(half + lax.rem(y + 4 - d, 4) * 64, 64)
        spread(base_y, src, 64, ysend, yrecv, 2 + d, ypeer(d)).wait_recv()
    back.append(spread(half, half, 256, csend, crecv, 1, sibling))
    back[-1].start()

    items_arrive(1)
    for src, dst in ((items2, item_out), (iacc2, iacc_out)):
        stores.append(pltpu.make_async_copy(src, dst, store.at[len(stores)]))
        stores[-1].start()

    spread(half, away, 256, csend, crecv, 1, sibling).wait_recv()
    mean_grad = total[...] * (1.0 / (NB * ROUNDS))
    step, racc_next = relation_rows(mean_grad, rcol[:, 0:1])
    ugown[...] = step
    rcol[...] = jnp.broadcast_to(racc_next, (D, 128))
    to_rows(rcol, racc)
    for src, dst in ((ugown, step_out), (racc, racc_out)):
        stores.append(pltpu.make_async_copy(src, dst, store.at[len(stores)]))

    for turn in range(ROUNDS):
        for k in range(UH // UC):
            user_copy(turn, k, own, own).wait_send()
            grad_copy(turn, k).wait_send()
        for k in range(IH // IC):

            @pl.when(core == 0)
            def _():
                item_copy_wide(turn, k, itabs[turn]).wait_send()

            @pl.when(core == 1)
            def _():
                item_copy(turn, k).wait_send()

        accum_copy(turn, iaccs[turn]).wait_send()
    for copy in [core_copy] + y_copies + z_copies + x_sends + back:
        copy.wait_send()
    for copy in stores[4:]:
        copy.start()
    for copy in stores:
        copy.wait()


def relation_rows(mean_grad, accum):
    accum_next = accum + jnp.mean(mean_grad * mean_grad, axis=1, keepdims=True)
    return mean_grad * lax.rsqrt(accum_next + epsilon), accum_next


def per_device(user_table, user_accum, item_table, item_accum, relation, relation_accum, targets):
    V = pltpu.VMEM
    dma = lambda *shape: pltpu.SemaphoreType.DMA(shape)
    shapes = [
        ((UH, D), F32), ((4, 128), F32), ((IH, D), F32), ((8, 128), F32), ((D, D), F32), ((4, 128), F32),
    ]
    outs = pl.pallas_call(
        kernel,
        out_shape=[jax.ShapeDtypeStruct(s, t) for s, t in shapes],
        in_specs=[pl.BlockSpec(memory_space=pl.ANY)] * 7,
        out_specs=[pl.BlockSpec(memory_space=pl.ANY)] * 6,
        scratch_shapes=[
            V((UH, D), F32), V((4, 128), F32), V((IH, D), F32), V((IH, D), F32), V((IH, D), F32),
            V((8, 128), F32), V((8, 128), F32), V((8, 128), F32), V((D, D), BF), V((4, 128), F32),
            V((2 * UH, IH), BF), V((2 * UH, IH), BF),
            V((2 * UH, D), BF), V((2 * UH, D), BF), V((IH, D), BF), V((IH, D), BF), V((IH, D), BF),
            V((IH, D), BF), V((IH, D), BF), V((2 * UH, D), BF), V((2 * UH, IH), BF),
            V((2 * UH, D), BF), V((UH, D), F32),
            V((UH, D), BF), V((UH, D), BF), V((UH, D), BF), V((UH, D), BF),
            V((UH, 128), F32), V((IH, 128), F32), V((D, 128), F32), V((D, D), F32),
            V((256, D), F32), V((3, 64, D), F32), V((7, 8, D), F32), V((4, 8, D), F32), V((D, D), F32),
            dma(8), dma(6), dma(2, 4), dma(2, 4), dma(2, 4), dma(2, 4), dma(2, 4), dma(2, 4), dma(2), dma(2),
            dma(2), dma(2), dma(6), dma(6), dma(14), dma(14), dma(3), dma(3),
        ],
        compiler_params=pltpu.CompilerParams(
            collective_id=0, has_side_effects=True, vmem_limit_bytes=60 * 2**20
        ),
    )(
        user_table, user_accum.reshape(4, 128), item_table, item_accum.reshape(8, 128),
        relation, relation_accum.reshape(4, 128), targets,
    )
    users, uacc, items, iacc, step, racc = outs
    return users, uacc.reshape(UH), items, iacc.reshape(IH), step, racc.reshape(D)


def solution(mesh):
    return jax.shard_map(
        per_device,
        mesh=mesh,
        in_specs=(
            P(("blk", "rel"), None),
            P(("blk", "rel")),
            P(("blk", "rel"), None),
            P(("blk", "rel")),
            P(),
            P(),
            P(None, "blk", "rel"),
        ),
        out_specs=(
            P(("blk", "rel"), None),
            P(("blk", "rel")),
            P(("blk", "rel"), None),
            P(("blk", "rel")),
            P(),
            P(),
        ),
        check_vma=False,
    )
```

time: 429 us -> 112 us (0.26)
  waiting for transfers between devices: 320 us -> 0 us
  Pallas kernels: 0 us -> 104 us
  matrix products: 41.4 us -> 0 us
  other arithmetic: 22.8 us -> 0 us
  starting transfers between devices: 19.2 us -> 0 us
  between operations: 14.2 us -> 0.66 us
    psum x1 -> x0, waiting for transfers between devices: 215 us -> none  [per_device(): total = lax.psum(relation_local, ('blk', 'rel'))]
    pallas_call x0 -> x1, Pallas kernels: none -> 104 us  [per_device(): pl.pallas_call(kernel, out_shape=[jax.ShapeDtypeStruct(s, t) for s, t in...]
    all_to_all x4 -> x0, waiting for transfers between devices: 66.4 us -> none  [the longest x2 44.8 us: sum_at_owner(): lax.all_to_all(in_blocks(shard, dim, peers), axis, 0, 0, tiled=True)]
    dot_general x10 -> x0, matrix products: 41.4 us -> none  [the longest x2 10.9 us: per_device(): term = jnp.dot(crossed, item_bf, preferred_element_type=jnp.float32)]
    ppermute x4 -> x0, waiting for transfers between devices: 38.8 us -> none  [from_behind(): lax.ppermute(shard, axis, [(i, (i + by) % peers) for i in range(peers)])]
    all_to_all x4 -> x0, starting transfers between devices: 18.8 us -> none  [the longest x2 9.91 us: sum_at_owner(): lax.all_to_all(in_blocks(shard, dim, peers), axis, 0, 0, tiled=True)]
    sub x3 -> x0, other arithmetic: 10.1 us -> none  [adagrad_rows(): table - learn_rate * grads * lax.rsqrt(accum_next + epsilon)[:, None]]
    reduce_sum x5 -> x0, other arithmetic: 7.67 us -> none  [the longest x2 4.75 us: sum_at_owner(): return jnp.sum(pieces, axis=0)]
  transfers between devices with their start and end apart: 9 -> 0, of which waited for: 5 -> 0; matrix products, arithmetic and copies ran while one was open for 12% -> 0% of each run, Pallas kernels for 0% -> 0%
where the time goes in v1:
time: 112 us; the launch traced here: 111 us
  Pallas kernels  104 us (93%)
  local copies, waits for them, and re-layouts  6.51 us (6%)
    pallas_call x1, Pallas kernels, per_device(): pl.pallas_call(kernel, out_shape=[jax.ShapeDtypeStruct(s, t) for s, t in...  104 us
    unnamed x16, local copies, waits for them, and re-layouts  6.51 us

profile of v1, /device:TPU:2, one launch (start us, length us, event | category | flops | bytes accessed | tf_op | source)
XLA Modules:
  0.0 111.1 jit_solution(2463662041746772470)
XLA Ops:
  0.6 103.9 %shard_map.118 = (f32[512,512]{1,0:T(8,128)}, f32[4,128]{1,0:T(4,128)}, f32[1024,512]{1,0:T(8,128)}, f32[8,128]{1,0:T(8,128)}, f32[512,512]{1,0:T(8,128)}, /*index=5*/f32[4,128]{1,0:T(4,128)}) custom-call(f32[512,512]{1,0:T(8,128)} %user_in.1, f32[4,128]{1,0:T(4,128)} %bitcast.8, f32[1024,512]{1,0:T(8,128)} %item_in.1, f32[8,128]{1,0:T(8,128)} %bitcast.6, ...), custom_call_target="tpu_custom_call" | custom-call | tf_op jit(solution)/shard_map/pallas_call | solution.py:379
  104.6 0.0 copy-start.4
  104.6 0.0 copy-start
  104.6 2.4 %copy.19 = f32[512,512]{1,0:T(8,128)} copy(f32[512,512]{1,0:T(8,128)} %get-tuple-element.24) | data formatting | bytes 2097152
  107.0 0.0 copy-done.4
  107.0 0.6 copy.20
  107.6 0.0 copy-done
  107.6 0.0 copy-start.2
  107.6 0.0 copy-start.1
  107.6 1.3 %copy.21 = f32[1024,512]{1,0:T(8,128)} copy(f32[1024,512]{1,0:T(8,128)S(1)} %copy-done) | data formatting | bytes 4194304
  108.9 0.0 copy-done.2
  108.9 0.0 copy-start.3
  108.9 0.6 copy.22
  109.5 0.0 copy-done.1
  109.5 1.0 copy.23
  110.5 0.0 copy-done.3
  110.5 0.6 copy.24
Async XLA Ops:
  104.6 2.4 %copy-start.4 = (f32[4,128]{1,0:T(4,128)S(1)}, f32[4,128]{1,0:T(4,128)}, u32[]{:S(2)}) copy-start(f32[4,128]{1,0:T(4,128)} %get-tuple-element.13) | copy-start | bytes 6148
  104.6 3.0 %copy-start = (f32[1024,512]{1,0:T(8,128)S(1)}, f32[1024,512]{1,0:T(8,128)}, u32[]{:S(2)}) copy-start(f32[1024,512]{1,0:T(8,128)} %get-tuple-element.26) | copy-start | bytes 6291460
  107.6 1.3 %copy-start.2 = (f32[8,128]{1,0:T(8,128)S(1)}, f32[8,128]{1,0:T(8,128)}, u32[]{:S(2)}) copy-start(f32[8,128]{1,0:T(8,128)} %get-tuple-element.15) | copy-start | bytes 12292
  107.6 2.0 %copy-start.1 = (f32[512,512]{1,0:T(8,128)S(1)}, f32[512,512]{1,0:T(8,128)}, u32[]{:S(2)}) copy-start(f32[512,512]{1,0:T(8,128)} %get-tuple-element.28) | copy-start | bytes 3145732
  108.9 1.6 %copy-start.3 = (f32[4,128]{1,0:T(4,128)S(1)}, f32[4,128]{1,0:T(4,128)}, u32[]{:S(2)}) copy-start(f32[4,128]{1,0:T(4,128)} %get-tuple-element.17) | copy-start | bytes 6148

commit v2 on v1

--- a/solution.py
+++ b/solution.py
@@ -18,6 +18,8 @@
 IC = 256
 BF = jnp.bfloat16
 F32 = jnp.float32
+SCATTER = F32
+GATHER = F32
 
 
 def mm(a, b, ca, cb):
@@ -40,12 +42,12 @@
 
 
 def kernel(
-    user_in, uacc_in, item_in, iacc_in, rel_in, racc_in, tgt_in,
-    user_out, uacc_out, item_out, iacc_out, step_out, racc_out,
-    users, uacc, items0, items1, items2, iacc0, iacc1, iacc2, rel, racc, tgt0, tgt1,
+    user_in, uacc_in, item_in, iacc_in, rel_in, tgt_in,
+    user_out, uacc_out, item_out, iacc_out, total_out,
+    users, uacc, items0, items1, items2, iacc0, iacc1, iacc2, rel, tgt0, tgt1,
     ub0, ub1, vb0, vb1, vb2, vtx0, vtx1, anchor, errors, wsum, ugown,
-    gtx0, gtx1, grx0, grx1, ucol, icol, rcol, term, rcore, ry, rz, rx, total,
-    load, store, usend, urecv, gsend, grecv, isend, irecv, asend, arecv,
+    gtx0, gtx1, grx0, grx1, ucol, icol, term, rcore, mine, ry, sumy, rz, rx, sumz, total,
+    load, usend, urecv, gsend, grecv, isend, irecv, asend, arecv,
     csend, crecv, ysend, yrecv, zsend, zrecv, xsend, xrecv,
 ):
     b = lax.axis_index("blk")
@@ -79,7 +81,7 @@
     loads = []
     for src, dst in (
         (user_in, users), (rel_in, rel), (item_in, items0), (tgt_in.at[0], tgt0),
-        (uacc_in, uacc), (iacc_in, iacc0), (racc_in, racc), (tgt_in.at[1], tgt1),
+        (uacc_in, uacc), (iacc_in, iacc0), (tgt_in.at[1], tgt1),
     ):
         copy = pltpu.make_async_copy(src, dst, load.at[len(loads)])
         copy.start()
@@ -160,7 +162,7 @@
         part = mm(ubs[turn][rows, :], wsum[rows, :], 0, 0)
         term[...] = part if first else term[...] + part
 
-    def item_chunk(turn, k):
+    def item_update(turn, k):
         rows = pl.ds(k * IC, IC)
         grad = mm(errors[:, k * IC : (k + 1) * IC], anchor[...], 0, 0)
         new, acc = adagrad(itabs[turn][rows, :], icol[rows, 0:1], grad)
@@ -168,6 +170,7 @@
         itabs[turn][rows, :] = new
         vtxs[turn][rows, :] = new.astype(BF)
 
+    def item_send(turn, k):
         @pl.when(core == 0)
         def _():
             item_copy_wide(turn, k, itabs[turn]).start()
@@ -218,22 +221,22 @@
     pl.semaphore_wait(barrier, len(greet))
     for k in range(UH // UC):
         user_copy(0, k, own, own).start()
-    for copy in loads[1:7]:
+    for copy in loads[1:6]:
         copy.wait()
     vb0[...] = items0[...].astype(BF)
     to_columns(uacc, ucol)
     to_columns(iacc0, icol)
-    to_columns(racc, rcol)
     own_rows(0)
     add_term(0, own, True)
     far_rows(0)
     for k in range(IH // IC):
-        item_chunk(0, k)
+        item_update(0, k)
+        item_send(0, k)
     to_rows(icol, iacc0)
     accum_copy(0, iacc0).start()
     user_chunks(0)
     add_term(0, far, False)
-    loads[7].wait()
+    loads[6].wait()
 
     items_arrive(0)
     to_columns(iacc1, icol)
@@ -244,103 +247,121 @@
 
     half = pl.multiple_of(core * 256, 256)
     away = pl.multiple_of(256 - core * 256, 256)
-    base_y = pl.multiple_of(half + y * 64, 64)
-    base_z = pl.multiple_of(base_y + z * 8, 8)
-
-    core_copy = pltpu.make_async_remote_copy(
-        term.at[pl.ds(away, 256)], rcore, csend.at[0], crecv.at[0],
-        device_id=sibling, device_id_type=MESH,
-    )
-    core_copy.start()
-    item_chunk(1, 0)
-    core_copy.wait_recv()
-    term[pl.ds(half, 256), :] = term[pl.ds(half, 256), :] + rcore[...]
-    y_copies = []
-    for d in range(1, 4):
-        piece = pl.multiple_of(half + lax.rem(y + d, 4) * 64, 64)
-        y_copies.append(pltpu.make_async_remote_copy(
-            term.at[pl.ds(piece, 64)], ry.at[d - 1], ysend.at[d - 1], yrecv.at[d - 1],
-            device_id=ypeer(d), device_id_type=MESH,
-        ))
-        y_copies[-1].start()
-    item_chunk(1, 1)
-    item_chunk(1, 2)
-    for copy in y_copies:
-        copy.wait_recv()
-    term[pl.ds(base_y, 64), :] = term[pl.ds(base_y, 64), :] + ry[0] + ry[1] + ry[2]
-    z_copies = []
-    for d in range(1, 8):
-        piece = pl.multiple_of(base_y + lax.rem(z + d, 8) * 8, 8)
-        z_copies.append(pltpu.make_async_remote_copy(
-            term.at[pl.ds(piece, 8)], rz.at[d - 1], zsend.at[d - 1], zrecv.at[d - 1],
-            device_id=zpeer(d), device_id_type=MESH,
-        ))
-        z_copies[-1].start()
-    item_chunk(1, 3)
+    base_y = pl.multiple_of(y * 64, 64)
+    base_z = pl.multiple_of(z * 8, 8)
+    started = []
+
+    def remote(src, dst, sends, recvs, k, peer):
+        return pltpu.make_async_remote_copy(
+            src, dst, sends.at[k], recvs.at[k], device_id=peer, device_id_type=MESH
+        )
+
+    def go(copies):
+        for copy in copies:
+            copy.start()
+        started.extend(copies)
+        return copies
+
+    halves = range(2)
+    cols = [pl.ds(h * 256, 256) for h in halves]
+    core_in = go([
+        remote(term.at[pl.ds(away, 256), cols[h]], rcore.at[:, cols[h]], csend, crecv, h, sibling)
+        for h in halves
+    ])
+    item_update(1, 0)
+    item_send(1, 0)
+    y_in = []
+    for h in halves:
+        core_in[h].wait_recv()
+        both = term[pl.ds(half, 256), cols[h]] + rcore[:, cols[h]]
+        mine[:, cols[h]] = both.astype(mine.dtype)
+        y_in.append(go([
+            remote(
+                mine.at[pl.ds(pl.multiple_of(lax.rem(y + d, 4) * 64, 64), 64), cols[h]],
+                ry.at[d - 1, :, cols[h]], ysend, yrecv, 3 * h + d - 1, ypeer(d),
+            )
+            for d in range(1, 4)
+        ]))
+    item_update(1, 1)
+    item_send(1, 1)
+    item_update(1, 2)
+    item_update(1, 3)
     to_rows(icol, iacc1)
     accum_copy(1, iacc1).start()
-    for copy in z_copies:
-        copy.wait_recv()
-    part = term[pl.ds(base_z, 8), :]
-    for d in range(7):
-        part = part + rz[d]
-    rx[pl.ds(x, 1)] = part[None]
-    x_sends, x_recvs = [], []
-    for d in range(1, 4):
-        args = dict(send_sem=xsend.at[d - 1], recv_sem=xrecv.at[d - 1],
-                    device_id=xpeer(d), device_id_type=MESH)
-        x_sends.append(pltpu.make_async_remote_copy(rx.at[x], rx.at[x], **args))
-        x_recvs.append(pltpu.make_async_remote_copy(rx.at[x], rx.at[lax.rem(x + 4 - d, 4)], **args))
-        x_sends[-1].start()
-
+    z_in = []
+    for h in halves:
+        for copy in y_in[h]:
+            copy.wait_recv()
+        part = mine[pl.ds(base_y, 64), cols[h]].astype(F32)
+        for d in range(3):
+            part = part + ry[d, :, cols[h]].astype(F32)
+        sumy[:, cols[h]] = part
+        z_in.append(go([
+            remote(
+                sumy.at[pl.ds(pl.multiple_of(lax.rem(z + d, 8) * 8, 8), 8), cols[h]],
+                rz.at[d - 1, :, cols[h]], zsend, zrecv, 7 * h + d - 1, zpeer(d),
+            )
+            for d in range(1, 8)
+        ]))
+    x_in = []
+    for h in halves:
+        for copy in z_in[h]:
+            copy.wait_recv()
+        part = sumy[pl.ds(base_z, 8), cols[h]]
+        for d in range(7):
+            part = part + rz[d, :, cols[h]]
+        rx[pl.ds(x, 1), :, cols[h]] = part[None]
+        go([
+            remote(rx.at[x, :, cols[h]], rx.at[x, :, cols[h]], xsend, xrecv, 3 * h + d - 1, xpeer(d))
+            for d in range(1, 4)
+        ])
+        x_in.append([
+            remote(
+                rx.at[x, :, cols[h]], rx.at[lax.rem(x + 4 - d, 4), :, cols[h]],
+                xsend, xrecv, 3 * h + d - 1, xpeer(d),
+            )
+            for d in range(1, 4)
+        ])
+    item_send(1, 2)
+    item_send(1, 3)
     user_chunks(1)
     to_rows(ucol, uacc)
-    stores = [
-        pltpu.make_async_copy(users, user_out, store.at[0]),
-        pltpu.make_async_copy(uacc, uacc_out, store.at[1]),
-    ]
-    for copy in stores:
-        copy.start()
-
-    for copy in x_recvs:
-        copy.wait_recv()
-    total[pl.ds(base_z, 8), :] = rx[0] + rx[1] + rx[2] + rx[3]
-
-    def spread(src0, dst0, n, sends, recvs, k, peer):
-        return pltpu.make_async_remote_copy(
-            total.at[pl.ds(src0, n)], total.at[pl.ds(dst0, n)], sends.at[k], recvs.at[k],
-            device_id=peer, device_id_type=MESH,
-        )
-
-    back = []
-    for d in range(1, 8):
-        back.append(spread(base_z, base_z, 8, zsend, zrecv, 6 + d, zpeer(d)))
-        back[-1].start()
-    for d in range(1, 8):
-        src = pl.multiple_of(base_y + lax.rem(z + 8 - d, 8) * 8, 8)
-        spread(base_z, src, 8, zsend, zrecv, 6 + d, zpeer(d)).wait_recv()
-    for d in range(1, 4):
-        back.append(spread(base_y, base_y, 64, ysend, yrecv, 2 + d, ypeer(d)))
-        back[-1].start()
-    for d in range(1, 4):
-        src = pl.multiple_of(half + lax.rem(y + 4 - d, 4) * 64, 64)
-        spread(base_y, src, 64, ysend, yrecv, 2 + d, ypeer(d)).wait_recv()
-    back.append(spread(half, half, 256, csend, crecv, 1, sibling))
-    back[-1].start()
-
+
+    def spread(buf, src0, dst0, n, h, sends, recvs, k, peer):
+        return remote(buf.at[pl.ds(src0, n), cols[h]], buf.at[pl.ds(dst0, n), cols[h]], sends, recvs, k, peer)
+
+    for h in halves:
+        for copy in x_in[h]:
+            copy.wait_recv()
+        sumz[pl.ds(base_z, 8), cols[h]] = rx[0, :, cols[h]] + rx[1, :, cols[h]] + rx[2, :, cols[h]] + rx[3, :, cols[h]]
+        go([
+            spread(sumz, base_z, base_z, 8, h, zsend, zrecv, 14 + 7 * h + d - 1, zpeer(d))
+            for d in range(1, 8)
+        ])
+    mine_y = pl.multiple_of(half + base_y, 64)
+    for h in halves:
+        for d in range(1, 8):
+            src = pl.multiple_of(lax.rem(z + 8 - d, 8) * 8, 8)
+            spread(sumz, base_z, src, 8, h, zsend, zrecv, 14 + 7 * h + d - 1, zpeer(d)).wait_recv()
+        total[pl.ds(mine_y, 64), cols[h]] = sumz[:, cols[h]].astype(total.dtype)
+        go([
+            spread(total, mine_y, mine_y, 64, h, ysend, yrecv, 6 + 3 * h + d - 1, ypeer(d))
+            for d in range(1, 4)
+        ])
+    for h in halves:
+        for d in range(1, 4):
+            src = pl.multiple_of(half + lax.rem(y + 4 - d, 4) * 64, 64)
+            spread(total, mine_y, src, 64, h, ysend, yrecv, 6 + 3 * h + d - 1, ypeer(d)).wait_recv()
+        go([spread(total, half, half, 256, h, csend, crecv, 2 + h, sibling)])
+
+    user_out[...] = users[...]
+    uacc_out[...] = uacc[...]
     items_arrive(1)
-    for src, dst in ((items2, item_out), (iacc2, iacc_out)):
-        stores.append(pltpu.make_async_copy(src, dst, store.at[len(stores)]))
-        stores[-1].start()
-
-    spread(half, away, 256, csend, crecv, 1, sibling).wait_recv()
-    mean_grad = total[...] * (1.0 / (NB * ROUNDS))
-    step, racc_next = relation_rows(mean_grad, rcol[:, 0:1])
-    ugown[...] = step
-    rcol[...] = jnp.broadcast_to(racc_next, (D, 128))
-    to_rows(rcol, racc)
-    for src, dst in ((ugown, step_out), (racc, racc_out)):
-        stores.append(pltpu.make_async_copy(src, dst, store.at[len(stores)]))
+    item_out[...] = items2[...]
+    iacc_out[...] = iacc2[...]
+    for h in halves:
+        spread(total, half, away, 256, h, csend, crecv, 2 + h, sibling).wait_recv()
+    total_out[...] = total[...]
 
     for turn in range(ROUNDS):
         for k in range(UH // UC):
@@ -357,51 +378,78 @@
                 item_copy(turn, k).wait_send()
 
         accum_copy(turn, iaccs[turn]).wait_send()
-    for copy in [core_copy] + y_copies + z_copies + x_sends + back:
+    for copy in started:
         copy.wait_send()
-    for copy in stores[4:]:
+
+
+def finish(users, uacc, items, iacc, total, racc, user_out, uacc_out, item_out, iacc_out, step_out, racc_out,
+           step, accum, rcol, sems):
+    copies = [
+        pltpu.make_async_copy(src, dst, sems.at[k])
+        for k, (src, dst) in enumerate((
+            (items, item_out), (users, user_out), (uacc, uacc_out), (iacc, iacc_out),
+            (step, step_out), (accum, racc_out),
+        ))
+    ]
+    for copy in copies[:4]:
         copy.start()
-    for copy in stores:
+    to_columns(racc, rcol)
+    mean_grad = total[...].astype(F32) * (1.0 / (NB * ROUNDS))
+    accum_next = rcol[:, 0:1] + jnp.mean(mean_grad * mean_grad, axis=1, keepdims=True)
+    step[...] = mean_grad * lax.rsqrt(accum_next + epsilon)
+    copies[4].start()
+    rcol[...] = jnp.broadcast_to(accum_next, (D, 128))
+    to_rows(rcol, accum)
+    copies[5].start()
+    for copy in copies:
         copy.wait()
-
-
-def relation_rows(mean_grad, accum):
-    accum_next = accum + jnp.mean(mean_grad * mean_grad, axis=1, keepdims=True)
-    return mean_grad * lax.rsqrt(accum_next + epsilon), accum_next
 
 
 def per_device(user_table, user_accum, item_table, item_accum, relation, relation_accum, targets):
     V = pltpu.VMEM
     dma = lambda *shape: pltpu.SemaphoreType.DMA(shape)
-    shapes = [
-        ((UH, D), F32), ((4, 128), F32), ((IH, D), F32), ((8, 128), F32), ((D, D), F32), ((4, 128), F32),
-    ]
+    vmem = pl.BlockSpec(memory_space=pltpu.VMEM)
+    hbm = pl.BlockSpec(memory_space=pltpu.HBM)
+    shapes = [((UH, D), F32), ((4, 128), F32), ((IH, D), F32), ((8, 128), F32)]
     outs = pl.pallas_call(
         kernel,
-        out_shape=[jax.ShapeDtypeStruct(s, t) for s, t in shapes],
-        in_specs=[pl.BlockSpec(memory_space=pl.ANY)] * 7,
-        out_specs=[pl.BlockSpec(memory_space=pl.ANY)] * 6,
+        out_shape=[jax.ShapeDtypeStruct(s, t) for s, t in shapes + [((D, D), GATHER)]],
+        in_specs=[hbm] * 6,
+        out_specs=[vmem] * 5,
         scratch_shapes=[
             V((UH, D), F32), V((4, 128), F32), V((IH, D), F32), V((IH, D), F32), V((IH, D), F32),
-            V((8, 128), F32), V((8, 128), F32), V((8, 128), F32), V((D, D), BF), V((4, 128), F32),
+            V((8, 128), F32), V((8, 128), F32), V((8, 128), F32), V((D, D), BF),
             V((2 * UH, IH), BF), V((2 * UH, IH), BF),
             V((2 * UH, D), BF), V((2 * UH, D), BF), V((IH, D), BF), V((IH, D), BF), V((IH, D), BF),
             V((IH, D), BF), V((IH, D), BF), V((2 * UH, D), BF), V((2 * UH, IH), BF),
             V((2 * UH, D), BF), V((UH, D), F32),
             V((UH, D), BF), V((UH, D), BF), V((UH, D), BF), V((UH, D), BF),
-            V((UH, 128), F32), V((IH, 128), F32), V((D, 128), F32), V((D, D), F32),
-            V((256, D), F32), V((3, 64, D), F32), V((7, 8, D), F32), V((4, 8, D), F32), V((D, D), F32),
-            dma(8), dma(6), dma(2, 4), dma(2, 4), dma(2, 4), dma(2, 4), dma(2, 4), dma(2, 4), dma(2), dma(2),
-            dma(2), dma(2), dma(6), dma(6), dma(14), dma(14), dma(3), dma(3),
+            V((UH, 128), F32), V((IH, 128), F32), V((D, D), F32),
+            V((256, D), F32), V((256, D), SCATTER), V((3, 64, D), SCATTER), V((64, D), F32), V((7, 8, D), F32),
+            V((4, 8, D), F32), V((64, D), F32), V((D, D), GATHER),
+            dma(7), dma(2, 4), dma(2, 4), dma(2, 4), dma(2, 4), dma(2, 4), dma(2, 4), dma(2), dma(2),
+            dma(4), dma(4), dma(12), dma(12), dma(28), dma(28), dma(6), dma(6),
         ],
         compiler_params=pltpu.CompilerParams(
-            collective_id=0, has_side_effects=True, vmem_limit_bytes=60 * 2**20
+            collective_id=0, has_side_effects=True, vmem_limit_bytes=48 * 2**20
         ),
     )(
-        user_table, user_accum.reshape(4, 128), item_table, item_accum.reshape(8, 128),
-        relation, relation_accum.reshape(4, 128), targets,
+        *(
+            pltpu.with_memory_space_constraint(v, pltpu.HBM)
+            for v in (
+                user_table, user_accum.reshape(4, 128), item_table, item_accum.reshape(8, 128),
+                relation, targets,
+            )
+        )
     )
-    users, uacc, items, iacc, step, racc = outs
+    users, uacc, items, iacc, step, racc = pl.pallas_call(
+        finish,
+        out_shape=[jax.ShapeDtypeStruct(s, t) for s, t in shapes + [((D, D), F32), ((4, 128), F32)]],
+        in_specs=[vmem] * 6,
+        out_specs=[hbm] * 6,
+        scratch_shapes=[V((D, D), F32), V((4, 128), F32), V((D, 128), F32), dma(6)],
+        compiler_params=pltpu.CompilerParams(vmem_limit_bytes=12 * 2**20),
+    )(*outs, relation_accum.reshape(4, 128))
     return users, uacc.reshape(UH), items, iacc.reshape(IH), step, racc.reshape(D)
 
 

time: 112 us -> 100 us (0.89)
  local copies, waits for them, and re-layouts: 6.51 us -> 0.01 us
  Pallas kernels: 104 us -> 98 us
    pallas_call x1, Pallas kernels: 104 us -> 95.9 us  [per_device(): pl.pallas_call(kernel, out_shape=[jax.ShapeDtypeStruct(s, t) for s, t in...]
    unnamed x16 -> x2, local copies, waits for them, and re-layouts: 6.51 us -> 0.01 us
    pallas_call x0 -> x1, Pallas kernels: none -> 2.08 us  [per_device(): pl.pallas_call(finish, out_shape=[jax.ShapeDtypeStruct(s, t) for s, t in...]
where the time goes in v2:
time: 100 us; the launch traced here: 98.7 us
  Pallas kernels  98 us (98%)
    pallas_call x1, Pallas kernels, per_device(): pl.pallas_call(kernel, out_shape=[jax.ShapeDtypeStruct(s, t) for s, t in...  95.9 us
    pallas_call x1, Pallas kernels, per_device(): pl.pallas_call(finish, out_shape=[jax.ShapeDtypeStruct(s, t) for s, t in...  2.08 us

profile of v2, /device:TPU:2, one launch (start us, length us, event | category | flops | bytes accessed | tf_op | source)
XLA Modules:
  0.0 98.7 jit_solution(6230483376161702928)
XLA Ops:
  0.6 0.0 copy-start
  0.6 95.9 %shard_map.118 = (f32[512,512]{1,0:T(8,128)S(1)}, f32[4,128]{1,0:T(4,128)S(1)}, f32[1024,512]{1,0:T(8,128)S(1)}, f32[8,128]{1,0:T(8,128)S(1)}, f32[512,512]{1,0:T(8,128)S(1)}) custom-call(f32[512,512]{1,0:T(8,128)} %user_in.1, f32[4,128]{1,0:T(4,128)} %bitcast.8, f32[1024,512]{1,0:T(8,128)} %item_in.1, f32[8,128]{1,0:T(8,128)} %bitcast.7, ...), custom_call_target="tpu_custom_call" | custom-call | tf_op jit(solution)/shard_map/pallas_call | solution.py:414
  96.6 0.0 copy-done
  96.6 2.1 %shard_map.119 = (f32[512,512]{1,0:T(8,128)}, f32[4,128]{1,0:T(4,128)}, f32[1024,512]{1,0:T(8,128)}, f32[8,128]{1,0:T(8,128)}, f32[512,512]{1,0:T(8,128)}, /*index=5*/f32[4,128]{1,0:T(4,128)}) custom-call(f32[512,512]{1,0:T(8,128)S(1)} %get-tuple-element.17.users, f32[4,128]{1,0:T(4,128)S(1)} %get-tuple-element.18.uacc, ...), custom_call_target="tpu_custom_call" | custom-call | tf_op jit(solution)/shard_map/pallas_call | solution.py:445
Async XLA Ops:
  0.6 96.0 %copy-start = (f32[512]{0:T(512)S(1)}, f32[512]{0:T(512)}, u32[]{:S(2)}) copy-start(f32[512]{0:T(512)} %param.12) | copy-start | bytes 6148

commit v3 on v2

--- a/solution.py
+++ b/solution.py
@@ -18,8 +18,8 @@
 IC = 256
 BF = jnp.bfloat16
 F32 = jnp.float32
-SCATTER = F32
-GATHER = F32
+SCATTER = BF
+GATHER = BF
 
 
 def mm(a, b, ca, cb):
@@ -323,9 +323,6 @@
             for d in range(1, 4)
         ])
     item_send(1, 2)
-    item_send(1, 3)
-    user_chunks(1)
-    to_rows(ucol, uacc)
 
     def spread(buf, src0, dst0, n, h, sends, recvs, k, peer):
         return remote(buf.at[pl.ds(src0, n), cols[h]], buf.at[pl.ds(dst0, n), cols[h]], sends, recvs, k, peer)
@@ -338,6 +335,7 @@
             spread(sumz, base_z, base_z, 8, h, zsend, zrecv, 14 + 7 * h + d - 1, zpeer(d))
             for d in range(1, 8)
         ])
+    item_send(1, 3)
     mine_y = pl.multiple_of(half + base_y, 64)
     for h in halves:
         for d in range(1, 8):
@@ -348,14 +346,16 @@
             spread(total, mine_y, mine_y, 64, h, ysend, yrecv, 6 + 3 * h + d - 1, ypeer(d))
             for d in range(1, 4)
         ])
+    user_chunks(1)
+    to_rows(ucol, uacc)
+    user_out[...] = users[...]
+    uacc_out[...] = uacc[...]
     for h in halves:
         for d in range(1, 4):
             src = pl.multiple_of(half + lax.rem(y + 4 - d, 4) * 64, 64)
             spread(total, mine_y, src, 64, h, ysend, yrecv, 6 + 3 * h + d - 1, ypeer(d)).wait_recv()
         go([spread(total, half, half, 256, h, csend, crecv, 2 + h, sibling)])
 
-    user_out[...] = users[...]
-    uacc_out[...] = uacc[...]
     items_arrive(1)
     item_out[...] = items2[...]
     iacc_out[...] = iacc2[...]

time: 100 us -> 95.2 us (0.952)
  Pallas kernels: 98 us -> 93.8 us
    pallas_call x1, Pallas kernels: 95.9 us -> 91.7 us  [per_device(): pl.pallas_call(kernel, out_shape=[jax.ShapeDtypeStruct(s, t) for s, t in...]
where the time goes in v3:
time: 95.2 us; the launch traced here: 94.5 us
  Pallas kernels  93.8 us (99%)
    pallas_call x1, Pallas kernels, per_device(): pl.pallas_call(kernel, out_shape=[jax.ShapeDtypeStruct(s, t) for s, t in...  91.7 us
    pallas_call x1, Pallas kernels, per_device(): pl.pallas_call(finish, out_shape=[jax.ShapeDtypeStruct(s, t) for s, t in...  2.07 us

profile of v3, /device:TPU:2, one launch (start us, length us, event | category | flops | bytes accessed | tf_op | source)
XLA Modules:
  0.0 94.5 jit_solution(2685213144447214538)
XLA Ops:
  0.6 0.0 copy-start
  0.6 91.7 %shard_map.118 = (f32[512,512]{1,0:T(8,128)S(1)}, f32[4,128]{1,0:T(4,128)S(1)}, f32[1024,512]{1,0:T(8,128)S(1)}, f32[8,128]{1,0:T(8,128)S(1)}, bf16[512,512]{1,0:T(8,128)(2,1)S(1)}) custom-call(f32[512,512]{1,0:T(8,128)} %user_in.1, f32[4,128]{1,0:T(4,128)} %bitcast.8, f32[1024,512]{1,0:T(8,128)} %item_in.1, f32[8,128]{1,0:T(8,128)} %bitcast.7, ...), custom_call_target="tpu_custom_call" | custom-call | tf_op jit(solution)/shard_map/pallas_call | solution.py:414
  92.4 0.0 copy-done
  92.4 2.1 %shard_map.119 = (f32[512,512]{1,0:T(8,128)}, f32[4,128]{1,0:T(4,128)}, f32[1024,512]{1,0:T(8,128)}, f32[8,128]{1,0:T(8,128)}, f32[512,512]{1,0:T(8,128)}, /*index=5*/f32[4,128]{1,0:T(4,128)}) custom-call(f32[512,512]{1,0:T(8,128)S(1)} %get-tuple-element.17.users, f32[4,128]{1,0:T(4,128)S(1)} %get-tuple-element.18.uacc, ...), custom_call_target="tpu_custom_call" | custom-call | tf_op jit(solution)/shard_map/pallas_call | solution.py:445
Async XLA Ops:
  0.6 91.8 %copy-start = (f32[512]{0:T(512)S(1)}, f32[512]{0:T(512)}, u32[]{:S(2)}) copy-start(f32[512]{0:T(512)} %param.12) | copy-start | bytes 6148
